TPU v7x, 32 devices: a whole 2x2x4 slice. The times are simulated.
32 devices in a mesh: row: 2 (over core), col: 8 (over z, x), grp: 2 (over y).
Axes of the slice: x: 2, y: 2, z: 4, core: 2. Of those that a mesh axis runs over, the one named last changes fastest.
Arguments:
- momentum: float32 [2, 4096, 16384], P('grp', 'row', 'col'), may hold values from -6 to 6
- gradient: bfloat16 [2, 4096, 16384], P('grp', 'row', 'col'), may hold values from -6 to 6
- factor_q: float32 [2, 16384, 256], P('grp', 'col', 'row'), may hold values from -0.046875 to 0.046875
- weights: float32 [2, 4096, 16384], P(None, 'row', ('col', 'grp')), may hold values from -6 to 6
- tokens: bfloat16 [256, 4096], P(None, 'row'), may hold values from -0.08984375 to 0.08984375
Outputs:
- momentum_out: float32 [2, 4096, 16384], P('grp', 'row', 'col')
- factor_out: float32 [2, 16384, 256], P('grp', 'col', 'row')
- weights_out: float32 [2, 4096, 16384], P(None, 'row', ('col', 'grp'))
- hidden: bfloat16 [256, 16384], P('row', ('col', 'grp'))
All inputs are finite; a program needn't handle non-finite values.
Results may differ from a plain program's by a relative error of at most 0.0061.
Values may be sent and summed in bfloat16 or wider, within the bound.
No kernel may reach another device: no remote copies, remote signals or barrier semaphores. Data moves between devices by JAX's collectives and lax.ppermute only.
A program may use at most 128 MiB of HBM per device.

v0:
```python
import math
import jax
import jax.numpy as jnp
from jax import lax
from jax.sharding import PartitionSpec as P

D = 4096
HID = 16384
feedback = 0.05
epsilon = 1e-06


def gram_of(left_rows):
    return jnp.dot(left_rows.T, left_rows, precision=lax.Precision.HIGHEST)


def orthonormal(gram_sum, left_rows):
    factor_l = jnp.linalg.cholesky(gram_sum)
    return jax.scipy.linalg.solve_triangular(factor_l, left_rows.T, lower=True).T


def local(momentum, gradient, factor_q, weights, tokens):
    buffer = momentum[0] + gradient[0].astype(jnp.float32)
    buffer_h = buffer.astype(jnp.bfloat16)
    partial_value = jnp.dot(
        buffer_h,
        lax.all_gather(factor_q[0].astype(jnp.bfloat16), "row", axis=1, tiled=True),
        preferred_element_type=jnp.float32,
    )
    left_full = lax.psum(partial_value, "col")
    gram_sum = lax.psum(gram_of(left_full), "row")
    left_h = orthonormal(gram_sum, left_full).astype(jnp.bfloat16)
    right_part = lax.dot_general(
        buffer_h, left_h, (((0,), (0,)), ((), ())), preferred_element_type=jnp.float32
    )
    rank_share = factor_q.shape[2]
    right_full = lax.psum(right_part, "row")
    squares = lax.psum(jnp.sum(right_full * right_full, axis=0), "col")
    new_q = right_full / jnp.sqrt(squares + epsilon)
    q_share = lax.dynamic_slice_in_dim(new_q, lax.axis_index("row") * rank_share, rank_share, 1)
    right_h = right_full.astype(jnp.bfloat16)
    new_q_h = new_q.astype(jnp.bfloat16)
    feedback_term = lax.dot_general(
        left_h, right_h, (((1,), (1,)), ((), ())), preferred_element_type=jnp.float32
    )
    mom_new = buffer - feedback * feedback_term
    left_both = lax.all_gather(left_h[None], "grp", axis=0, tiled=True)
    right_both = lax.all_to_all(new_q_h[None], "grp", split_axis=1, concat_axis=0, tiled=True)
    step_size = 0.4 * math.sqrt(max(D, HID))
    low_rank = lax.dot_general(
        left_both, right_both, (((2,), (2,)), ((0,), (0,))), preferred_element_type=jnp.float32
    )
    new_weights = weights - step_size * low_rank
    weights_h = new_weights.astype(jnp.bfloat16)
    dec_parts = lax.psum_scatter(
        jnp.einsum("bd,pdh->bph", tokens, weights_h, preferred_element_type=jnp.float32),
        "row",
        scatter_dimension=0,
        tiled=True,
    )
    hidden = (jax.nn.silu(dec_parts[:, 0]) * dec_parts[:, 1]).astype(jnp.bfloat16)
    return (mom_new[None], q_share[None], new_weights, hidden)


def solution(mesh):
    in_specs = (
        P("grp", "row", "col"),
        P("grp", "row", "col"),
        P("grp", "col", "row"),
        P(None, "row", ("col", "grp")),
        P(None, "row"),
    )
    out_specs = (
        P("grp", "row", "col"),
        P("grp", "col", "row"),
        P(None, "row", ("col", "grp")),
        P("row", ("col", "grp")),
    )
    return jax.shard_map(local, mesh=mesh, in_specs=in_specs, out_specs=out_specs, check_vma=False)
```

profile of v0, /device:TPU:0, one launch (start us, length us, event | category | flops | bytes accessed | tf_op | source)
XLA Modules:
  0.0 394.4 jit_solution(15597743867390131542)
XLA Ops:
  7.2 2.1 convert_element_type.31
  9.4 12.2 %all-gather.5.cloned.1.call-done = bf16[1,2048,256]{2,1,0:T(8,128)(2,1)} async-done(((bf16[1,2048,128]{2,1,0:T(8,128)(2,1)}), bf16[1,2048,256]{2,1,0:T(8,128)(2,1)}) %all-gather.5.cloned.1.call-update) | async-done | bytes 1048592 | tf_op jit(solution)/shard_map/all_gather | solution.py:27
  21.6 12.3 %fusion.9 = f32[2048,256]{1,0:T(8,128)} fusion(bf16[1,2048,256]{2,1,0:T(8,128)(2,1)} %all-gather.5.cloned.1.call-done, f32[1,2048,2048]{2,1,0:T(8,128)} %param.5, bf16[1,2048,2048]{2,1,0:T(8,128)(2,1)} %param.6), kind=kOutput, calls=%fused_computation.18 | convolution fusion | flops 2160066560 | bytes 28311552 | tf_op jit(solution)/shard_map/dot_general | solution.py:25
  34.0 103.6 %all-reduce.5.cloned.1.call-done = f32[2048,256]{1,0:T(8,128)} async-done(((f32[2048,256]{1,0:T(8,128)}), f32[2048,256]{1,0:T(8,128)}) %all-reduce.5.cloned.1.call-update) | async-done | bytes 2097168 | tf_op jit(solution)/shard_map/psum | solution.py:30
  137.6 6.4 %fusion.25 = f32[256,256]{0,1:T(8,128)} fusion(f32[2048,256]{1,0:T(8,128)} %all-reduce.5.cloned.1.call-done), kind=kOutput, calls=%fused_computation.56 | convolution fusion | flops 1610612736 | bytes 2359296 | tf_op jit(solution)/shard_map/dot_general | solution.py:14
  144.0 0.3 all-reduce.9.cloned.1.call-start
  144.3 17.3 %all-reduce.7.cloned.1.call-done = f32[256,256]{0,1:T(8,128)} async-done(((f32[256,256]{0,1:T(8,128)}), f32[256,256]{0,1:T(8,128)}) %all-reduce.7.cloned.1.call-update) | async-done | bytes 262160 | tf_op jit(solution)/shard_map/psum | solution.py:31
  161.6 1.1 copy.21
  162.7 1.0 fusion.16
  163.7 0.7 copy-done.10
  164.4 11.7 %cholesky.50 = f32[128,128]{1,0:T(8,128)S(1)} custom-call(f32[128,128]{1,0:T(8,128)S(1)} %cholesky.118), custom_call_target="Cholesky" | custom-call | tf_op jit(solution)/shard_map/jit(cholesky)/cholesky | solution.py:18
  176.2 9.8 %custom-call.15 = f32[1,128,128]{1,2,0:T(8,128)S(1)} custom-call(f32[1,128,128]{2,1,0:T(8,128)S(1)} %get-tuple-element.39), custom_call_target="InvertDiagBlocksLowerTriangular" | custom-call | tf_op jit(solution)/shard_map/jit(cholesky)/cholesky | solution.py:18
  186.0 1.0 constant_dynamic-update-slice_fusion
  187.0 1.1 convolution_subtract_fusion.1
  188.2 11.7 %cholesky.105 = f32[128,128]{1,0:T(8,128)S(1)} custom-call(f32[128,128]{1,0:T(8,128)S(1)} %convolution_subtract_fusion.1), custom_call_target="Cholesky" | custom-call | tf_op jit(solution)/shard_map/jit(cholesky)/cholesky | solution.py:18
  199.9 0.7 compare_reduce_fusion
  202.0 1.0 select_select_fusion
  203.0 5.7 %while.1 = (s32[]{:T(128)}, f32[256,256]{1,0:T(8,128)S(1)}, s32[2,2]{1,0:T(2,128)S(1)}, f32[2,128,128]{2,1,0:T(8,128)}, s32[]{:T(128)}) while((s32[]{:T(128)}, f32[256,256]{1,0:T(8,128)S(1)}, s32[2,2]{1,0:T(2,128)S(1)}, f32[2,128,128]{2,1,0:T(8,128)}, s32[]{:T(128)}) %tuple.32), condition=%wide.while_cond, body=%wide.while_body.sunk | while | flops 2 | bytes 132205 | solution.py:19
  203.5 0.6 fusion.35
  204.1 2.0 bitcast_dynamic-update-slice_fusion.2
  206.2 0.6 fusion.35
  206.7 2.0 bitcast_dynamic-update-slice_fusion.2
  208.8 20.5 %custom-call.16 = f32[2,128,128]{1,2,0:T(8,128)S(1)} custom-call(f32[2,128,128]{2,1,0:T(8,128)} %get-tuple-element.11), custom_call_target="InvertDiagBlocksLowerTriangular" | custom-call | tf_op jit(solution)/shard_map/jit(_solve_triangular)/triangular_solve | solution.py:19
  229.3 1.1 fusion.24
  230.3 1.8 convolution_subtract_fusion
  232.2 1.1 convolution_convert_fusion
  233.3 13.1 %fusion.15 = f32[2048,256]{1,0:T(8,128)} fusion(bf16[128,2048]{1,0:T(8,128)(2,1)S(1)} %convolution_convert_fusion, bf16[128,2048]{1,0:T(8,128)(2,1)S(1)} %get-tuple-element.42, f32[1,2048,2048]{2,1,0:T(8,128)} %param.5, bf16[1,2048,2048]{2,1,0:T(8,128)(2,1)} %param.6), kind=kOutput, calls=%fused_computation.29 | convolution fusion | flops 2162163712 | bytes 28311552 | tf_op jit(solution)/shard_map/dot_general | solution.py:33
  246.5 1.0 copy-done.6
  247.4 1.0 fusion.14
  248.5 20.6 %all-reduce.9.cloned.1.call-done = f32[2048,256]{1,0:T(8,128)} async-done(((f32[2048,256]{1,0:T(8,128)}), f32[2048,256]{1,0:T(8,128)}) %all-reduce.9.cloned.1.call-update) | async-done | bytes 2097168 | tf_op jit(solution)/shard_map/psum | solution.py:37
  269.1 2.0 multiply_reduce_fusion
  271.1 21.8 %psum.31 = f32[256]{0:T(256)S(1)} all-reduce(f32[256]{0:T(256)S(1)} %multiply_reduce_fusion), channel_id=1, replica_groups=mesh['row'=2,'col'=8,'grp'=2] {'col'}, use_global_device_ids=true, to_apply=%region_8.9 | all-reduce | flops 256 | bytes 2048 | tf_op jit(solution)/shard_map/psum | solution.py:38
  292.9 1.5 convert_bitcast_fusion
  294.4 12.9 %copy.33 = bf16[1,2048,256]{2,0,1:T(2,128)(2,1)} copy(bf16[1,2048,256]{2,1,0:T(8,128)(2,1)S(1)} %get-tuple-element.32) | data formatting | bytes 2097152 | tf_op jit(solution)/shard_map/broadcast_in_dim | solution.py:48
  307.3 0.5 broadcast.117
  307.8 12.6 %reduce.12 = bf16[2048,256]{1,0:T(8,128)(2,1)} reduce(bf16[2048,1,256]{2,1,0:T(2,128)(2,1)} %bitcast.81, bf16[]{:T(256)} %broadcast.117), dimensions={1}, to_apply=%bitcast.70.reduce_sub_computation | reduce | bytes 2097154
  320.5 2.2 reshape.56
  322.6 4.4 %all-to-all-start = ((bf16[2,2,131072]{2,1,0:T(2,128)(2,1)}), bf16[2,2,131072]{2,1,0:T(2,128)(2,1)}, u32[]{:S(2)}, u32[]{:S(2)}) async-start(bf16[2,2,131072]{2,1,0:T(2,128)(2,1)} %reshape.56), calls=%async_computation | async-start | bytes 2097152 | tf_op jit(solution)/shard_map/all_to_all | solution.py:48
  327.1 4.3 %copy.30 = bf16[4096,256]{1,0:T(8,128)(2,1)} copy(bf16[4096,256]{0,1:T(8,128)(2,1)} %all-gather.7.cloned.1.call-done) | data formatting | bytes 4194304 | tf_op jit(solution)/shard_map/all_gather | solution.py:47
  331.4 6.3 %all-to-all-done = bf16[2,2,131072]{2,1,0:T(2,128)(2,1)} async-done(((bf16[2,2,131072]{2,1,0:T(2,128)(2,1)}), bf16[2,2,131072]{2,1,0:T(2,128)(2,1)}, u32[]{:S(2)}, u32[]{:S(2)}) %all-to-all-start) | async-done | bytes 1048608 | tf_op jit(solution)/shard_map/all_to_all | solution.py:48
  337.7 3.0 reshape.57
  340.7 1.9 copy.31
  342.9 14.3 %multiply_subtract_fusion = f32[2,2048,1024]{2,1,0:T(8,128)} fusion(f32[2,2048,1024]{2,1,0:T(8,128)} %param.8, bf16[2,2048,256]{2,1,0:T(8,128)(2,1)S(1)} %bitcast.79, bf16[2,1024,256]{2,1,0:T(8,128)(2,1)S(1)} %bitcast.82), kind=kOutput, calls=%fused_computation.5 | convolution fusion | flops 2155872256 | bytes 36700160 | tf_op jit(solution)/shard_map/dot_general | solution.py:50
  357.2 9.6 %fusion.3 = f32[256,2,1024]{0,2,1:T(8,128)} fusion(f32[2,2048,1024]{2,1,0:T(8,128)} %multiply_subtract_fusion, bf16[256,2048]{1,0:T(8,128)(2,1)S(1)} %copy-done), kind=kOutput, calls=%fused_computation.12 | convolution fusion | flops 2151677952 | bytes 19922944 | tf_op jit(solution)/shard_map/bd,pdh->bph/dot_general | solution.py:56
  366.9 2.4 dynamic-slice_bitcast_fusion
  369.2 15.9 %fusion = f32[1,2048,2048]{2,1,0:T(8,128)} fusion(f32[1,2048,2048]{2,1,0:T(8,128)} %param.5, bf16[1,2048,2048]{2,1,0:T(8,128)(2,1)} %param.6, f32[2048,256]{1,0:T(8,128)S(1)} %copy-done.1, bf16[128,2048]{1,0:T(8,128)(2,1)S(1)} %copy-done.4, bf16[128,2048]{1,0:T(8,128)(2,1)S(1)} %copy-done.7), kind=kOutput, calls=%fused_computation.4 | convolution fusion | flops 2166882304 | bytes 45088768 | tf_op jit(solution)/shard_map/dot_general | solution.py:43
  385.1 1.3 fusion.13
  386.4 0.9 copy.26
  (43 shorter events, 0.9 us)
Async XLA Ops:
  7.2 350.1 %copy-start = (bf16[256,2048]{1,0:T(8,128)(2,1)S(1)}, bf16[256,2048]{1,0:T(8,128)(2,1)}, u32[]{:S(2)}) copy-start(bf16[256,2048]{1,0:T(8,128)(2,1)} %param.9) | copy-start | bytes 3145732
  7.2 14.5 %all-gather.5.cloned.1.call-start = ((), (), s32[]{:S(2)}) async-start(), calls=%async_computation.6 | async-start | bytes 1572864 | tf_op jit(solution)/shard_map/all_gather | solution.py:27
  9.4 128.2 %all-reduce.5.cloned.1.call-start = ((), (), s32[]{:S(2)}) async-start(), calls=%async_computation.2 | async-start | bytes 4194304 | tf_op jit(solution)/shard_map/psum | solution.py:30
  33.9 127.7 %all-reduce.7.cloned.1.call-start = ((), (), s32[]{:S(2)}) async-start(), calls=%async_computation.3 | async-start | bytes 524288 | tf_op jit(solution)/shard_map/psum | solution.py:31
  143.9 85.3 %copy-start.2 = (f32[2048,256]{1,0:T(8,128)S(1)}, f32[2048,256]{1,0:T(8,128)}, u32[]{:S(2)}) copy-start(f32[2048,256]{1,0:T(8,128)} %all-reduce.5.cloned.1.call-done) | copy-start | bytes 6291460
  144.0 125.1 %all-reduce.9.cloned.1.call-start = ((), (), s32[]{:S(2)}) async-start(), calls=%async_computation.4 | async-start | bytes 4194304 | tf_op jit(solution)/shard_map/psum | solution.py:37
  163.7 0.7 copy-start.10
  199.9 2.0 copy-start.9
  230.3 2.9 copy-start.5
  233.3 13.2 %copy-start.3 = (bf16[128,2048]{1,0:T(8,128)(2,1)}, bf16[128,2048]{1,0:T(8,128)(2,1)S(1)}, u32[]{:S(2)}) copy-start(bf16[128,2048]{1,0:T(8,128)(2,1)S(1)} %convolution_convert_fusion) | copy-start | bytes 1572868
  246.4 1.0 copy-start.6
  246.4 80.7 %all-gather.7.cloned.1.call-start = ((), (), s32[]{:S(2)}) async-start(), calls=%async_computation.7 | async-start | bytes 3145728 | tf_op jit(solution)/shard_map/all_gather | solution.py:47
  269.1 23.8 %copy-start.1 = (f32[2048,256]{1,0:T(8,128)S(1)}, f32[2048,256]{1,0:T(8,128)}, u32[]{:S(2)}) copy-start(f32[2048,256]{1,0:T(8,128)} %all-reduce.9.cloned.1.call-done) | copy-start | bytes 6291460
  322.6 15.1 %all-to-all-start = ((bf16[2,2,131072]{2,1,0:T(2,128)(2,1)}), bf16[2,2,131072]{2,1,0:T(2,128)(2,1)}, u32[]{:S(2)}, u32[]{:S(2)}) async-start(bf16[2,2,131072]{2,1,0:T(2,128)(2,1)} %reshape.56), calls=%async_computation | async-start | bytes 2097152 | tf_op jit(solution)/shard_map/all_to_all | solution.py:48
  327.1 58.0 %reduce-scatter.2.cloned.1.call-start = ((), (), s32[]{:S(2)}) async-start(), calls=%async_computation.5 | async-start | bytes 3145728 | tf_op jit(solution)/shard_map/reduce_scatter | solution.py:55
  340.7 2.2 copy-start.8
  366.8 2.4 copy-start.4
  366.9 2.4 copy-start.7
Sparse Core Ops, SparseCore 0:
  10.1 11.4 all-gather.4
  34.0 103.4 all-reduce.4
  144.1 17.4 all-reduce.6
  246.5 22.4 all-reduce.8
  271.0 34.2 all-gather.6
  367.0 5.6 reduce-scatter.1
where the time goes:
time: 400 us; the launch traced here: 394 us
  waiting for transfers between devices  160 us (40%)
  matrix products  77.6 us (19%)
  other arithmetic  77.2 us (19%)
  local copies, waits for them, and re-layouts  36.3 us (9%)
  blocking collectives  21.8 us (5%)
  between operations  15.9 us (4%)
  starting transfers between devices  4.96 us (1%)
    psum x1, waiting for transfers between devices, local(): left_full = lax.psum(partial_value, 'col')  104 us
    another operation x6, other arithmetic, orthonormal(): factor_l = jnp.linalg.cholesky(gram_sum)  34 us
    psum x1, blocking collectives, local(): squares = lax.psum(jnp.sum(right_full * right_full, axis=0), 'col')  21.8 us
    another operation x3, other arithmetic, orthonormal(): jax.scipy.linalg.solve_triangular(factor_l, left_rows.T, lower=True)  21.5 us
    psum x1, waiting for transfers between devices, local(): right_full = lax.psum(right_part, 'row')  20.6 us
    psum x1, waiting for transfers between devices, local(): gram_sum = lax.psum(gram_of(left_full), 'row')  17.3 us
    dot_general x1, matrix products, local(): lax.dot_general(left_h, right_h, (((1,), (1,)), ((), ())), preferred_elem...  15.9 us
    dot_general x1, matrix products, local(): lax.dot_general(left_both, right_both, (((2,), (2,)), ((0,), (0,))), pref...  14.3 us
  transfers between devices with their start and end apart: 7, of which 5 were waited for; matrix products, arithmetic and copies ran while one was open for 14% of the time, Pallas kernels for 0%

commit v1 on v0

--- a/solution.py
+++ b/solution.py
@@ -27,7 +27,8 @@
         lax.all_gather(factor_q[0].astype(jnp.bfloat16), "row", axis=1, tiled=True),
         preferred_element_type=jnp.float32,
     )
-    left_full = lax.psum(partial_value, "col")
+    shards = lax.all_gather(partial_value, "col", axis=0, tiled=False)
+    left_full = shards.sum(axis=0)
     gram_sum = lax.psum(gram_of(left_full), "row")
     left_h = orthonormal(gram_sum, left_full).astype(jnp.bfloat16)
     right_part = lax.dot_general(

time: 400 us -> 526 us (1.31)
  waiting for transfers between devices: 160 us -> 283 us
  other arithmetic: 77.2 us -> 83 us
    all_gather x0 -> x1, waiting for transfers between devices: none -> 229 us  [local(): shards = lax.all_gather(partial_value, 'col', axis=0, tiled=False)]
    psum x1 -> x0, waiting for transfers between devices: 104 us -> none  [local(): left_full = lax.psum(partial_value, 'col')]
    reduce_sum x0 -> x1, other arithmetic: none -> 7.14 us  [local(): left_full = shards.sum(axis=0)]
  transfers between devices with their start and end apart: 7 -> 7, of which waited for: 5 -> 5; matrix products, arithmetic and copies ran while one was open for 14% -> 11% of each run, Pallas kernels for 0% -> 0%
where the time goes in v1:
time: 526 us; the launch traced here: 519 us
  waiting for transfers between devices  283 us (54%)
  other arithmetic  83 us (16%)
  matrix products  75.5 us (14%)
  local copies, waits for them, and re-layouts  35.2 us (7%)
  blocking collectives  21.8 us (4%)
  between operations  15.8 us (3%)
    all_gather x1, waiting for transfers between devices, local(): shards = lax.all_gather(partial_value, 'col', axis=0, tiled=False)  229 us
    another operation x6, other arithmetic, orthonormal(): factor_l = jnp.linalg.cholesky(gram_sum)  33.9 us
    psum x1, blocking collectives, local(): squares = lax.psum(jnp.sum(right_full * right_full, axis=0), 'col')  21.8 us
    psum x1, waiting for transfers between devices, local(): right_full = lax.psum(right_part, 'row')  21.5 us
    another operation x3, other arithmetic, orthonormal(): jax.scipy.linalg.solve_triangular(factor_l, left_rows.T, lower=True)  20.2 us
    dot_general x1, matrix products, local(): lax.dot_general(left_h, right_h, (((1,), (1,)), ((), ())), preferred_elem...  15.9 us
    psum x1, waiting for transfers between devices, local(): gram_sum = lax.psum(gram_of(left_full), 'row')  14.4 us
    dot_general x1, matrix products, local(): lax.dot_general(left_both, right_both, (((2,), (2,)), ((0,), (0,))), pref...  14.3 us
  transfers between devices with their start and end apart: 7, of which 5 were waited for; matrix products, arithmetic and copies ran while one was open for 11% of the time, Pallas kernels for 0%

profile of v1, /device:TPU:0, one launch (start us, length us, event | category | flops | bytes accessed | tf_op | source)
XLA Modules:
  0.0 519.4 jit_solution(2016915493409201162)
XLA Ops:
  7.2 2.1 convert_element_type.31
  9.4 12.2 %all-gather.7.cloned.1.call-done = bf16[1,2048,256]{2,1,0:T(8,128)(2,1)} async-done(((bf16[1,2048,128]{2,1,0:T(8,128)(2,1)}), bf16[1,2048,256]{2,1,0:T(8,128)(2,1)}) %all-gather.7.cloned.1.call-update) | async-done | bytes 1048592 | tf_op jit(solution)/shard_map/all_gather | solution.py:27
  21.6 12.3 %fusion.9 = f32[2048,256]{1,0:T(8,128)} fusion(bf16[1,2048,256]{2,1,0:T(8,128)(2,1)} %all-gather.7.cloned.1.call-done, f32[1,2048,2048]{2,1,0:T(8,128)} %param.5, bf16[1,2048,2048]{2,1,0:T(8,128)(2,1)} %param.6), kind=kOutput, calls=%fused_computation.18 | convolution fusion | flops 2160066560 | bytes 28311552 | tf_op jit(solution)/shard_map/dot_general | solution.py:25
  34.0 228.6 %all-gather.9.cloned.1.call-done = f32[16384,256]{1,0:T(8,128)} async-done(((f32[2048,256]{1,0:T(8,128)}), f32[16384,256]{1,0:T(8,128)}) %all-gather.9.cloned.1.call-update) | async-done | bytes 16777232 | tf_op jit(solution)/shard_map/all_gather | solution.py:30
  262.6 7.1 %reduce_sum.18 = f32[2048,256]{1,0:T(8,128)S(1)} reduce(f32[8,2048,256]{2,1,0:T(8,128)} %bitcast.78, f32[]{:T(128)} %constant.87.clone.1), dimensions={0}, to_apply=%region_0.0 | reduce | flops 3670016 | bytes 18874372 | tf_op jit(solution)/shard_map/reduce_sum | solution.py:31
  269.7 4.2 fusion.25
  273.9 0.3 all-reduce.6.cloned.1.call-start
  274.2 1.8 copy.28
  276.1 14.4 %all-reduce.4.cloned.1.call-done = f32[256,256]{0,1:T(8,128)} async-done(((f32[256,256]{0,1:T(8,128)}), f32[256,256]{0,1:T(8,128)}) %all-reduce.4.cloned.1.call-update) | async-done | bytes 262160 | tf_op jit(solution)/shard_map/psum | solution.py:32
  290.4 1.1 copy.27
  291.5 1.0 fusion.16
  292.5 11.7 %cholesky.50 = f32[128,128]{1,0:T(8,128)S(1)} custom-call(f32[128,128]{1,0:T(8,128)S(1)} %cholesky.118), custom_call_target="Cholesky" | custom-call | tf_op jit(solution)/shard_map/jit(cholesky)/cholesky | solution.py:18
  304.3 9.8 %custom-call.15 = f32[1,128,128]{1,2,0:T(8,128)S(1)} custom-call(f32[1,128,128]{2,1,0:T(8,128)S(1)} %get-tuple-element.43), custom_call_target="InvertDiagBlocksLowerTriangular" | custom-call | tf_op jit(solution)/shard_map/jit(cholesky)/cholesky | solution.py:18
  314.1 0.2 constant_dynamic-update-slice_fusion
  314.3 0.3 convolution_subtract_fusion.1
  314.6 11.7 %cholesky.105 = f32[128,128]{1,0:T(8,128)S(1)} custom-call(f32[128,128]{1,0:T(8,128)S(1)} %convolution_subtract_fusion.1), custom_call_target="Cholesky" | custom-call | tf_op jit(solution)/shard_map/jit(cholesky)/cholesky | solution.py:18
  326.3 0.6 compare_reduce_fusion
  328.4 4.0 while.1
  328.4 0.6 fusion.35
  329.0 1.4 bitcast_dynamic-update-slice_fusion.2
  330.4 0.6 fusion.35
  331.0 1.4 bitcast_dynamic-update-slice_fusion.2
  332.4 20.2 %custom-call.16 = f32[2,128,128]{1,2,0:T(8,128)S(1)} custom-call(f32[2,128,128]{2,1,0:T(8,128)S(1)} %get-tuple-element.11), custom_call_target="InvertDiagBlocksLowerTriangular" | custom-call | tf_op jit(solution)/shard_map/jit(_solve_triangular)/triangular_solve | solution.py:19
  352.6 2.3 fusion.24
  354.9 2.4 convolution_subtract_fusion
  357.3 1.1 convolution_convert_fusion
  358.4 13.1 %fusion.15 = f32[2048,256]{1,0:T(8,128)} fusion(bf16[128,2048]{1,0:T(8,128)(2,1)S(1)} %convolution_convert_fusion, bf16[128,2048]{1,0:T(8,128)(2,1)S(1)} %get-tuple-element.46, f32[1,2048,2048]{2,1,0:T(8,128)} %param.5, bf16[1,2048,2048]{2,1,0:T(8,128)(2,1)} %param.6), kind=kOutput, calls=%fused_computation.29 | convolution fusion | flops 2162163712 | bytes 28311552 | tf_op jit(solution)/shard_map/dot_general | solution.py:34
  371.6 1.0 fusion.14
  372.6 21.5 %all-reduce.6.cloned.1.call-done = f32[2048,256]{1,0:T(8,128)} async-done(((f32[2048,256]{1,0:T(8,128)}), f32[2048,256]{1,0:T(8,128)}) %all-reduce.6.cloned.1.call-update) | async-done | bytes 2097168 | tf_op jit(solution)/shard_map/psum | solution.py:38
  394.2 2.0 multiply_reduce_fusion
  396.2 21.8 %psum.23 = f32[256]{0:T(256)S(1)} all-reduce(f32[256]{0:T(256)S(1)} %multiply_reduce_fusion), channel_id=1, replica_groups=mesh['row'=2,'col'=8,'grp'=2] {'col'}, use_global_device_ids=true, to_apply=%region_8.9 | all-reduce | flops 256 | bytes 2048 | tf_op jit(solution)/shard_map/psum | solution.py:39
  418.0 1.5 convert_bitcast_fusion
  419.5 12.9 %copy.38 = bf16[1,2048,256]{2,0,1:T(2,128)(2,1)} copy(bf16[1,2048,256]{2,1,0:T(8,128)(2,1)S(1)} %get-tuple-element.36) | data formatting | bytes 2097152 | tf_op jit(solution)/shard_map/broadcast_in_dim | solution.py:49
  432.4 0.5 broadcast.117
  432.9 12.6 %reduce.12 = bf16[2048,256]{1,0:T(8,128)(2,1)} reduce(bf16[2048,1,256]{2,1,0:T(2,128)(2,1)} %bitcast.83, bf16[]{:T(256)} %broadcast.117), dimensions={1}, to_apply=%bitcast.71.reduce_sub_computation | reduce | bytes 2097154
  445.5 2.2 reshape.57
  447.7 4.4 all-to-all-start
  452.2 4.3 copy.35
  456.5 6.3 %all-to-all-done = bf16[2,2,131072]{2,1,0:T(2,128)(2,1)} async-done(((bf16[2,2,131072]{2,1,0:T(2,128)(2,1)}), bf16[2,2,131072]{2,1,0:T(2,128)(2,1)}, u32[]{:S(2)}, u32[]{:S(2)}) %all-to-all-start) | async-done | bytes 1048608 | tf_op jit(solution)/shard_map/all_to_all | solution.py:49
  462.8 3.0 reshape.58
  465.7 1.9 copy.36
  467.6 0.3 copy-done.6
  467.9 14.3 %multiply_subtract_fusion = f32[2,2048,1024]{2,1,0:T(8,128)} fusion(f32[2,2048,1024]{2,1,0:T(8,128)} %param.8, bf16[2,2048,256]{2,1,0:T(8,128)(2,1)S(1)} %bitcast.79, bf16[2,1024,256]{2,1,0:T(8,128)(2,1)S(1)} %bitcast.84), kind=kOutput, calls=%fused_computation.5 | convolution fusion | flops 2155872256 | bytes 36700160 | tf_op jit(solution)/shard_map/dot_general | solution.py:51
  482.3 9.6 %fusion.3 = f32[256,2,1024]{0,2,1:T(8,128)} fusion(f32[2,2048,1024]{2,1,0:T(8,128)} %multiply_subtract_fusion, bf16[256,2048]{1,0:T(8,128)(2,1)S(1)} %copy-done), kind=kOutput, calls=%fused_computation.12 | convolution fusion | flops 2151677952 | bytes 19922944 | tf_op jit(solution)/shard_map/bd,pdh->bph/dot_general | solution.py:57
  491.9 2.4 dynamic-slice_bitcast_fusion
  494.2 15.9 %fusion = f32[1,2048,2048]{2,1,0:T(8,128)} fusion(f32[1,2048,2048]{2,1,0:T(8,128)} %param.5, bf16[1,2048,2048]{2,1,0:T(8,128)(2,1)} %param.6, f32[2048,256]{1,0:T(8,128)S(1)} %copy-done.1, bf16[128,2048]{1,0:T(8,128)(2,1)S(1)} %copy-done.3, bf16[128,2048]{1,0:T(8,128)(2,1)S(1)} %copy-done.5), kind=kOutput, calls=%fused_computation.4 | convolution fusion | flops 2166882304 | bytes 45088768 | tf_op jit(solution)/shard_map/dot_general | solution.py:44
  510.1 1.3 fusion.13
  511.5 0.9 copy.32
  (37 shorter events, 0.6 us)
Async XLA Ops:
  7.2 475.1 %copy-start = (bf16[256,2048]{1,0:T(8,128)(2,1)S(1)}, bf16[256,2048]{1,0:T(8,128)(2,1)}, u32[]{:S(2)}) copy-start(bf16[256,2048]{1,0:T(8,128)(2,1)} %param.9) | copy-start | bytes 3145732
  7.2 14.5 %all-gather.7.cloned.1.call-start = ((), (), s32[]{:S(2)}) async-start(), calls=%async_computation.5 | async-start | bytes 1572864 | tf_op jit(solution)/shard_map/all_gather | solution.py:27
  9.4 253.2 %all-gather.9.cloned.1.call-start = ((), (), s32[]{:S(2)}) async-start(), calls=%async_computation.6 | async-start | bytes 18874368 | tf_op jit(solution)/shard_map/all_gather | solution.py:30
  33.9 256.5 %all-reduce.4.cloned.1.call-start = ((), (), s32[]{:S(2)}) async-start(), calls=%async_computation.2 | async-start | bytes 524288 | tf_op jit(solution)/shard_map/psum | solution.py:32
  273.9 120.3 %all-reduce.6.cloned.1.call-start = ((), (), s32[]{:S(2)}) async-start(), calls=%async_computation.3 | async-start | bytes 4194304 | tf_op jit(solution)/shard_map/psum | solution.py:38
  354.9 16.7 %copy-start.4 = (bf16[128,2048]{1,0:T(8,128)(2,1)}, bf16[128,2048]{1,0:T(8,128)(2,1)S(1)}, u32[]{:S(2)}) copy-start(bf16[128,2048]{1,0:T(8,128)(2,1)S(1)} %get-tuple-element.46) | copy-start | bytes 1572868
  358.4 13.2 %copy-start.2 = (bf16[128,2048]{1,0:T(8,128)(2,1)}, bf16[128,2048]{1,0:T(8,128)(2,1)S(1)}, u32[]{:S(2)}) copy-start(bf16[128,2048]{1,0:T(8,128)(2,1)S(1)} %convolution_convert_fusion) | copy-start | bytes 1572868
  371.5 80.7 %all-gather.11.cloned.1.call-start = ((), (), s32[]{:S(2)}) async-start(), calls=%async_computation.7 | async-start | bytes 3145728 | tf_op jit(solution)/shard_map/all_gather | solution.py:48
  394.2 23.8 %copy-start.1 = (f32[2048,256]{1,0:T(8,128)S(1)}, f32[2048,256]{1,0:T(8,128)}, u32[]{:S(2)}) copy-start(f32[2048,256]{1,0:T(8,128)} %all-reduce.6.cloned.1.call-done) | copy-start | bytes 6291460
  447.7 15.1 %all-to-all-start = ((bf16[2,2,131072]{2,1,0:T(2,128)(2,1)}), bf16[2,2,131072]{2,1,0:T(2,128)(2,1)}, u32[]{:S(2)}, u32[]{:S(2)}) async-start(bf16[2,2,131072]{2,1,0:T(2,128)(2,1)} %reshape.57), calls=%async_computation | async-start | bytes 2097152 | tf_op jit(solution)/shard_map/all_to_all | solution.py:49
  452.1 58.0 %reduce-scatter.2.cloned.1.call-start = ((), (), s32[]{:S(2)}) async-start(), calls=%async_computation.4 | async-start | bytes 3145728 | tf_op jit(solution)/shard_map/reduce_scatter | solution.py:56
  465.7 2.2 copy-start.6
  491.9 2.4 copy-start.3
  491.9 2.4 copy-start.5
Sparse Core Ops, SparseCore 0:
  10.1 11.4 all-gather.6
  34.0 228.4 all-gather.8
  274.0 16.3 all-reduce.3
  371.6 22.4 all-reduce.5
  396.1 34.2 all-gather.10
  492.0 5.6 reduce-scatter.1
